TPU v7x, 32 devices: a whole 2x2x4 slice. The times are simulated.
32 devices in a mesh: groups: 1, blk: 16 (over z, y, x), head: 2 (over core).
Axes of the slice: x: 2, y: 2, z: 4, core: 2. Of those that a mesh axis runs over, the one named last changes fastest.
Arguments:
- queries: bfloat16 [128, 8192], P(('groups', 'blk'), 'head'), may hold values from -6 to 6
- key_cache: bfloat16 [2, 32768, 8, 128], P('groups', 'blk', 'head'), may hold values from -18 to 18
- value_cache: bfloat16 [2, 32768, 8, 128], P('groups', 'blk', 'head'), may hold values from -6 to 6
- lengths: int32 [2], P('groups'), may hold values from 0 to 32704
- residual: bfloat16 [128, 8192], P('groups', 'blk'), may hold values from -6 to 6
- out_weight: bfloat16 [8192, 8192], P('head', 'blk'), may hold values from -0.0625 to 0.0625
- norm_gain: bfloat16 [8192], P('blk'), may hold values from 0.099609375 to 1.8984375
- gate_weight: bfloat16 [8192, 16384], P(None, ('head', 'blk')), may hold values from -0.0625 to 0.0625
- up_weight: bfloat16 [8192, 16384], P(None, ('head', 'blk')), may hold values from -0.0625 to 0.0625
- down_weight: bfloat16 [16384, 8192], P('head', 'blk'), may hold values from -0.046875 to 0.046875
Outputs:
- layer_out: bfloat16 [128, 8192], P('groups', 'blk')
Inputs may be any that keep to these rules, and one draw needn't show every extreme that they name: lengths[b] + 64 <= 32768; the cache holds sequence b's new keys and values at positions lengths[b] to lengths[b] + 63.
All inputs are finite; a program needn't handle non-finite values.
Results may differ from a plain program's by a relative error of at most 0.01.
Values may be sent and summed in bfloat16 or wider, within the bound.
No kernel may reach another device: no remote copies, remote signals or barrier semaphores. Data moves between devices by JAX's collectives and lax.ppermute only.
A program may use at most 128 MiB of HBM per device.

v0:
```python
import jax
import jax.numpy as jnp
from jax import lax
from jax.sharding import PartitionSpec as P

D = 8192
neg_big = -1e30
epsilon = 1e-06


def body(
    queries,
    key_cache,
    value_cache,
    lengths,
    residual,
    out_weight,
    norm_gain,
    gate_weight,
    up_weight,
    down_weight,
):
    blocks = lax.axis_size("blk")
    my_block = lax.axis_index("blk")
    batch, ctx_dev, kv_local, head_dim = key_cache.shape
    rows_dev = queries.shape[0]
    rows_all = rows_dev * blocks
    new_tokens = rows_all // batch
    heads_local = queries.shape[1] // head_dim
    group_size = heads_local // kv_local
    all_queries = lax.all_gather(queries, "blk", axis=0, tiled=True)
    shaped = all_queries.reshape(batch, new_tokens, kv_local, group_size, head_dim)
    scores = jnp.einsum(
        "bqkgd,bckd->bqkgc", shaped, key_cache, preferred_element_type=jnp.float32
    ) * head_dim ** (-0.5)
    query_pos = lengths[:, None] + jnp.arange(new_tokens, dtype=jnp.int32)[None, :]
    key_pos = my_block * ctx_dev + jnp.arange(ctx_dev, dtype=jnp.int32)
    visible = key_pos[None, None, None, None, :] <= query_pos[:, :, None, None, None]
    block_max = jnp.max(jnp.where(visible, scores, neg_big), axis=-1)
    weights = jnp.where(visible, jnp.exp(scores - block_max[..., None]), 0.0)
    block_sum = jnp.sum(weights, axis=-1)
    block_out = jnp.einsum(
        "bqkgc,bckd->bqkgd",
        weights.astype(jnp.bfloat16),
        value_cache,
        preferred_element_type=jnp.float32,
    )
    block_mean = (block_out / jnp.maximum(block_sum, 1.0)[..., None]).astype(jnp.bfloat16)
    row_max = block_max.reshape(rows_all, heads_local)
    row_sum = block_sum.reshape(rows_all, heads_local)
    row_mean = block_mean.reshape(rows_all, heads_local, head_dim)
    got_max, got_sum = (
        lax.all_to_all(row_max[None], "blk", split_axis=1, concat_axis=0, tiled=True),
        lax.all_to_all(row_sum[None], "blk", split_axis=1, concat_axis=0, tiled=True),
    )
    got_mean = lax.all_to_all(row_mean[None], "blk", split_axis=1, concat_axis=0, tiled=True)
    top = jnp.max(got_max, axis=0)
    factor = got_sum * jnp.exp(got_max - top[None])
    total_sum = jnp.sum(factor, axis=0)
    total_out = jnp.sum(got_mean.astype(jnp.float32) * factor[..., None], axis=0)
    attn = (
        (total_out / total_sum[..., None])
        .astype(jnp.bfloat16)
        .reshape(rows_dev, heads_local * head_dim)
    )
    proj_part = jnp.dot(
        lax.all_gather(attn, "blk", axis=0, tiled=True),
        out_weight,
        preferred_element_type=jnp.float32,
    )
    projected = lax.psum(proj_part.astype(jnp.bfloat16), "head").astype(jnp.float32)
    stream = residual.astype(jnp.float32) + projected
    squares = lax.psum(jnp.sum(stream * stream, axis=1), "blk")
    normed = (
        stream * lax.rsqrt(squares / D + epsilon)[:, None] * norm_gain.astype(jnp.float32)[None, :]
    ).astype(jnp.bfloat16)
    piece = lax.all_gather(normed, "blk", axis=1, tiled=True)
    gate = jnp.dot(piece, gate_weight, preferred_element_type=jnp.float32)
    up = jnp.dot(piece, up_weight, preferred_element_type=jnp.float32)
    hidden = (jax.nn.silu(gate) * up).astype(jnp.bfloat16)
    down_part = jnp.dot(
        lax.all_gather(hidden, "blk", axis=1, tiled=True),
        down_weight,
        preferred_element_type=jnp.float32,
    )
    down_total = lax.psum(down_part.astype(jnp.bfloat16), "head").astype(jnp.float32)
    return (stream + down_total).astype(jnp.bfloat16)


def solution(mesh):
    in_specs = (
        P(("groups", "blk"), "head"),
        P("groups", "blk", "head", None),
        P("groups", "blk", "head", None),
        P("groups"),
        P("groups", "blk"),
        P("head", "blk"),
        P("blk"),
        P(None, ("head", "blk")),
        P(None, ("head", "blk")),
        P("head", "blk"),
    )
    out_specs = P("groups", "blk")
    return jax.shard_map(body, mesh=mesh, in_specs=in_specs, out_specs=out_specs, check_vma=False)
```

profile of v0, /device:TPU:0, one launch (start us, length us, event | category | flops | bytes accessed | tf_op | source)
XLA Modules:
  0.0 444.1 jit_solution(5362369163561286765)
XLA Ops:
  6.5 0.0 all-gather.5.cloned.1.call-start
  6.5 0.7 all-gather.5.cloned.1.call-update
  7.3 0.7 iota_add_fusion.1
  8.0 0.2 broadcast_compare_fusion
  8.2 59.7 %all-gather.5.cloned.1.call-done = bf16[128,4096]{1,0:T(8,128)(2,1)} async-done(((bf16[8,4096]{1,0:T(8,128)(2,1)}), bf16[128,4096]{1,0:T(8,128)(2,1)}) %all-gather.5.cloned.1.call-update) | async-done | bytes 1048592 | tf_op jit(solution)/shard_map/all_gather | solution.py:31
  67.9 1.5 copy.45
  69.4 17.1 %fusion = (f32[2,64,4,8]{1,3,2,0:T(8,128)S(1)}, f32[2,4,2048,64,8]{2,3,4,1,0:T(8,128)}) fusion(pred[2,64,2048]{2,1,0:T(8,128)(4,1)S(1)} %broadcast_compare_fusion, bf16[2,64,4,8,128]{4,3,2,1,0:T(8,128)(2,1)S(1)} %bitcast.53, bf16[2,2048,4,128,1]{3,2,1,0,4:T(4,128)(2,1)} %bitcast.55), kind=kOutput, calls=%fused_computation.2 | convolution fusion | flops 2172645376 | bytes 39075840 | tf_op jit(solution)/shard_map/bqkgd,bckd->bqkgc/dot_general | solution.py:33
  86.5 15.1 %fusion.3 = f32[2,64,4,8]{1,3,2,0:T(8,128)S(1)} fusion(f32[2,4,2048,64,8]{2,3,4,1,0:T(8,128)} %get-tuple-element.8, f32[2,64,4,8]{1,3,2,0:T(8,128)S(1)} %get-tuple-element.7, pred[2,64,2048]{2,1,0:T(8,128)(4,1)S(1)} %broadcast_compare_fusion), kind=kLoop, calls=%fused_computation.5 | loop fusion | flops 33550336 | bytes 33849344 | tf_op jit(solution)/shard_map/reduce_sum | solution.py:41
  101.6 0.1 broadcast_in_dim_reshape.11
  101.7 0.1 copy.38
  101.8 0.5 broadcast.58
  102.3 0.8 reduce.2
  103.1 0.7 reshape.82
  103.8 4.4 %all-to-all-start.2 = ((f32[16,1,256]{2,1,0:T(1,128)}), f32[16,1,256]{2,1,0:T(1,128)S(1)}, u32[]{:S(2)}, u32[]{:S(2)}) async-start(f32[16,1,256]{2,1,0:T(1,128)} %reshape.82), calls=%async_computation.2 | async-start | bytes 32768 | tf_op jit(solution)/shard_map/all_to_all | solution.py:53
  108.3 0.1 broadcast_in_dim_reshape.10
  108.4 0.1 copy.36
  108.5 0.8 reduce
  109.3 0.7 reshape.80
  110.0 5.6 %all-to-all-done.2 = f32[16,1,256]{2,1,0:T(1,128)S(1)} async-done(((f32[16,1,256]{2,1,0:T(1,128)}), f32[16,1,256]{2,1,0:T(1,128)S(1)}, u32[]{:S(2)}, u32[]{:S(2)}) %all-to-all-start.2) | async-done | bytes 16416 | tf_op jit(solution)/shard_map/all_to_all | solution.py:53
  115.6 3.5 all-to-all-start.1
  119.1 15.6 %fusion.12 = bf16[2,64,4,8,128]{4,1,3,2,0:T(8,128)(2,1)S(1)} fusion(bf16[2,2048,4,128,1]{3,2,1,0,4:T(4,128)(2,1)} %bitcast.63, f32[2,4,2048,64,8]{2,3,4,1,0:T(8,128)} %get-tuple-element.8, f32[2,64,4,8]{1,3,2,0:T(8,128)S(1)} %get-tuple-element.7, pred[2,64,2048]{2,1,0:T(8,128)(4,1)S(1)} %broadcast_compare_fusion, f32[2,64,4,8]{1,3,2,0:T(8,128)S(1)} %broadcast_maximum_fusion), kind=kOutput, calls=%fused_computation.15 | convolution fusion | flops 2182086656 | bytes 39092224 | tf_op jit(solution)/shard_map/bqkgc,bckd->bqkgd/dot_general | solution.py:42
  134.7 0.0 copy-start.3
  134.7 0.0 copy-start.1
  134.8 1.7 copy.33
  136.4 0.0 all-to-all-done.1
  136.4 6.9 %all-to-all-start = ((bf16[1,128,32,128]{3,2,0,1:T(8,128)(2,1)}), bf16[1,128,32,128]{3,2,0,1:T(8,128)(2,1)S(1)}, u32[]{:S(2)}, u32[]{:S(2)}) async-start(bf16[1,128,32,128]{3,2,0,1:T(8,128)(2,1)} %bitcast.5), calls=%async_computation | async-start | bytes 2097152 | tf_op jit(solution)/shard_map/all_to_all | solution.py:56
  143.3 0.2 all-gather.7.cloned.1.call-start
  143.5 0.6 reduce.3
  144.2 0.1 reshape.83
  144.3 0.6 reduce.1
  145.0 0.1 reshape.81
  145.2 19.7 %all-to-all-done = bf16[1,128,32,128]{3,2,0,1:T(8,128)(2,1)S(1)} async-done(((bf16[1,128,32,128]{3,2,0,1:T(8,128)(2,1)}), bf16[1,128,32,128]{3,2,0,1:T(8,128)(2,1)S(1)}, u32[]{:S(2)}, u32[]{:S(2)}) %all-to-all-start) | async-done | bytes 1048608 | tf_op jit(solution)/shard_map/all_to_all | solution.py:56
  164.9 0.7 fusion.11
  165.6 0.1 fusion.19
  165.8 0.7 copy.60
  166.4 0.0 all-gather.7.cloned.1.call-update
  166.4 0.0 all-reduce.3.cloned.1.call-start
  166.5 54.4 %all-gather.7.cloned.1.call-done = bf16[128,4096]{1,0:T(8,128)(2,1)} async-done(((bf16[8,4096]{1,0:T(8,128)(2,1)}), bf16[128,4096]{1,0:T(8,128)(2,1)}) %all-gather.7.cloned.1.call-update) | async-done | bytes 1048592 | tf_op jit(solution)/shard_map/all_gather | solution.py:67
  220.9 3.9 convolution_convert_fusion
  224.8 0.0 all-reduce.3.cloned.1.call-update
  224.8 0.0 all-gather.9.cloned.1.call-start
  224.8 0.0 copy-done.3
  224.9 16.8 %all-reduce.3.cloned.1.call-done = bf16[128,512]{1,0:T(8,128)(2,1)} async-done(((bf16[128,512]{1,0:T(8,128)(2,1)}), bf16[128,512]{1,0:T(8,128)(2,1)}) %all-reduce.3.cloned.1.call-update) | async-done | bytes 131088 | tf_op jit(solution)/shard_map/psum | solution.py:71
  241.7 0.0 copy-done.1
  241.7 1.0 multiply_reduce_fusion
  242.7 42.0 %psum.22 = f32[128]{0:T(128)S(1)} all-reduce(f32[128]{0:T(128)S(1)} %multiply_reduce_fusion), channel_id=1, replica_groups=mesh['groups'=1,'blk'=16,'head'=2] {'blk'}, use_global_device_ids=true, to_apply=%region_7.8 | all-reduce | flops 128 | bytes 1024 | tf_op jit(solution)/shard_map/psum | solution.py:73
  284.7 1.7 multiply_convert_fusion
  286.4 0.0 all-gather.9.cloned.1.call-update
  286.4 0.0 all-gather.11.cloned.1.call-start
  286.5 56.9 %all-gather.9.cloned.1.call-done = bf16[128,8192]{1,0:T(8,128)(2,1)} async-done(((bf16[128,512]{1,0:T(8,128)(2,1)}), bf16[128,8192]{1,0:T(8,128)(2,1)}) %all-gather.9.cloned.1.call-update) | async-done | bytes 2097168 | tf_op jit(solution)/shard_map/all_gather | solution.py:77
  343.3 0.0 copy-start
  343.3 5.4 %fusion.23 = f32[128,512]{1,0:T(8,128)S(1)} fusion(bf16[128,8192]{1,0:T(8,128)(2,1)} %all-gather.9.cloned.1.call-done, bf16[8192,512]{1,0:T(8,128)(2,1)} %param.17), kind=kOutput, calls=%fused_computation.37 | convolution fusion | flops 1073741824 | bytes 10747904 | tf_op jit(solution)/shard_map/dot_general | solution.py:78
  348.7 0.0 copy-done
  348.7 5.4 %fusion.17 = bf16[128,512]{1,0:T(8,128)(2,1)} fusion(bf16[128,8192]{1,0:T(8,128)(2,1)S(1)} %copy-done, bf16[8192,512]{1,0:T(8,128)(2,1)} %param.18, f32[128,512]{1,0:T(8,128)S(1)} %fusion.23), kind=kOutput, calls=%fused_computation.17 | convolution fusion | flops 1074135040 | bytes 10878976 | tf_op jit(solution)/shard_map/dot_general | solution.py:79
  354.2 0.0 all-gather.11.cloned.1.call-update
  354.2 0.0 copy-start.2
  354.2 0.0 all-reduce.5.cloned.1.call-start
  354.3 59.2 %all-gather.11.cloned.1.call-done = bf16[128,8192]{1,0:T(8,128)(2,1)} async-done(((bf16[128,512]{1,0:T(8,128)(2,1)}), bf16[128,8192]{1,0:T(8,128)(2,1)}) %all-gather.11.cloned.1.call-update) | async-done | bytes 2097168 | tf_op jit(solution)/shard_map/all_gather | solution.py:82
  413.4 5.9 %convolution_convert_fusion.1 = bf16[128,512]{1,0:T(8,128)(2,1)} fusion(bf16[128,8192]{1,0:T(8,128)(2,1)} %all-gather.11.cloned.1.call-done, bf16[8192,512]{1,0:T(8,128)(2,1)} %param.19), kind=kOutput, calls=%fused_computation.19 | convolution fusion | flops 1073807360 | bytes 10616832 | tf_op jit(solution)/shard_map/dot_general | solution.py:81
  419.4 0.0 all-reduce.5.cloned.1.call-update
  419.4 16.2 %all-reduce.5.cloned.1.call-done = bf16[128,512]{1,0:T(8,128)(2,1)} async-done(((bf16[128,512]{1,0:T(8,128)(2,1)}), bf16[128,512]{1,0:T(8,128)(2,1)}) %all-reduce.5.cloned.1.call-update) | async-done | bytes 131088 | tf_op jit(solution)/shard_map/psum | solution.py:86
  435.6 0.0 copy-done.2
  435.6 1.6 add_convert_fusion
  (8 shorter events, 0.1 us)
Async XLA Ops:
  6.5 61.4 %all-gather.5.cloned.1.call-start = ((), (), s32[]{:S(2)}) async-start(), calls=%async_computation.3 | async-start | bytes 1114112 | tf_op jit(solution)/shard_map/all_gather | solution.py:31
  103.8 11.8 %all-to-all-start.2 = ((f32[16,1,256]{2,1,0:T(1,128)}), f32[16,1,256]{2,1,0:T(1,128)S(1)}, u32[]{:S(2)}, u32[]{:S(2)}) async-start(f32[16,1,256]{2,1,0:T(1,128)} %reshape.82), calls=%async_computation.2 | async-start | bytes 32768 | tf_op jit(solution)/shard_map/all_to_all | solution.py:53
  115.6 20.8 %all-to-all-start.1 = ((f32[16,1,256]{2,1,0:T(1,128)}), f32[16,1,256]{2,1,0:T(1,128)S(1)}, u32[]{:S(2)}, u32[]{:S(2)}) async-start(f32[16,1,256]{2,1,0:T(1,128)} %reshape.80), calls=%async_computation.1 | async-start | bytes 32768 | tf_op jit(solution)/shard_map/all_to_all | solution.py:54
  134.7 90.1 %copy-start.3 = (bf16[512]{0:T(512)(128)(2,1)S(1)}, bf16[512]{0:T(512)(128)(2,1)}, u32[]{:S(2)}) copy-start(bf16[512]{0:T(512)(128)(2,1)} %param.16) | copy-start | bytes 3076
  134.7 106.9 %copy-start.1 = (bf16[128,512]{1,0:T(8,128)(2,1)S(1)}, bf16[128,512]{1,0:T(8,128)(2,1)}, u32[]{:S(2)}) copy-start(bf16[128,512]{1,0:T(8,128)(2,1)} %param.14) | copy-start | bytes 393220
  136.4 28.5 %all-to-all-start = ((bf16[1,128,32,128]{3,2,0,1:T(8,128)(2,1)}), bf16[1,128,32,128]{3,2,0,1:T(8,128)(2,1)S(1)}, u32[]{:S(2)}, u32[]{:S(2)}) async-start(bf16[1,128,32,128]{3,2,0,1:T(8,128)(2,1)} %bitcast.5), calls=%async_computation | async-start | bytes 2097152 | tf_op jit(solution)/shard_map/all_to_all | solution.py:56
  143.3 77.6 %all-gather.7.cloned.1.call-start = ((), (), s32[]{:S(2)}) async-start(), calls=%async_computation.4 | async-start | bytes 1114112 | tf_op jit(solution)/shard_map/all_gather | solution.py:67
  166.4 75.2 %all-reduce.3.cloned.1.call-start = ((), (), s32[]{:S(2)}) async-start(), calls=%async_computation.5 | async-start | bytes 262144 | tf_op jit(solution)/shard_map/psum | solution.py:71
  224.8 118.5 %all-gather.9.cloned.1.call-start = ((), (), s32[]{:S(2)}) async-start(), calls=%async_computation.6 | async-start | bytes 2228224 | tf_op jit(solution)/shard_map/all_gather | solution.py:77
  286.4 127.0 %all-gather.11.cloned.1.call-start = ((), (), s32[]{:S(2)}) async-start(), calls=%async_computation.7 | async-start | bytes 2228224 | tf_op jit(solution)/shard_map/all_gather | solution.py:82
  343.3 5.4 %copy-start = (bf16[128,8192]{1,0:T(8,128)(2,1)S(1)}, bf16[128,8192]{1,0:T(8,128)(2,1)}, u32[]{:S(2)}) copy-start(bf16[128,8192]{1,0:T(8,128)(2,1)} %all-gather.9.cloned.1.call-done) | copy-start | bytes 6291460
  354.2 81.4 %copy-start.2 = (bf16[128,512]{1,0:T(8,128)(2,1)S(1)}, bf16[128,512]{1,0:T(8,128)(2,1)}, u32[]{:S(2)}) copy-start(bf16[128,512]{1,0:T(8,128)(2,1)} %all-reduce.3.cloned.1.call-done) | copy-start | bytes 393220
  354.2 81.4 %all-reduce.5.cloned.1.call-start = ((), (), s32[]{:S(2)}) async-start(), calls=%async_computation.8 | async-start | bytes 262144 | tf_op jit(solution)/shard_map/psum | solution.py:86
Sparse Core Ops, SparseCore 0:
  10.1 57.7 all-gather.4
  166.6 54.2 all-gather.6
  224.9 16.7 all-reduce.2
  286.5 56.7 all-gather.8
  354.3 59.0 all-gather.10
  419.5 16.0 all-reduce.4
where the time goes:
time: 445 us; the launch traced here: 444 us
  waiting for transfers between devices  289 us (65%)
  matrix products  53.4 us (12%)
  blocking collectives  42 us (9%)
  other arithmetic  24 us (5%)
  starting transfers between devices  15.2 us (3%)
  between operations  13.7 us (3%)
  local copies, waits for them, and re-layouts  6.46 us (1%)
    all_gather x1, waiting for transfers between devices, body(): all_queries = lax.all_gather(queries, 'blk', axis=0, tiled=True)  59.7 us
    all_gather x1, waiting for transfers between devices, body(): lax.all_gather(hidden, 'blk', axis=1, tiled=True)  59.2 us
    all_gather x1, waiting for transfers between devices, body(): piece = lax.all_gather(normed, 'blk', axis=1, tiled=True)  56.9 us
    all_gather x1, waiting for transfers between devices, body(): lax.all_gather(attn, 'blk', axis=0, tiled=True)  54.4 us
    psum x1, blocking collectives, body(): squares = lax.psum(jnp.sum(stream * stream, axis=1), 'blk')  42 us
    all_to_all x1, waiting for transfers between devices, body(): lax.all_to_all(row_mean[None], 'blk', split_axis=1, concat_axis=0, tiled=...  19.7 us
    dot_general x1, matrix products, body(): jnp.einsum('bqkgd,bckd->bqkgc', shaped, key_cache, preferred_element_type...  17.1 us
    psum x1, waiting for transfers between devices, body(): lax.psum(proj_part.astype(jnp.bfloat16), 'head').astype(jnp.float32)  16.8 us
  transfers between devices with their start and end apart: 9, of which 8 were waited for; matrix products, arithmetic and copies ran while one was open for 5% of the time, Pallas kernels for 0%

commit v1 on v0

--- a/solution.py
+++ b/solution.py
@@ -6,6 +6,16 @@
 D = 8192
 neg_big = -1e30
 epsilon = 1e-06
+
+
+def collect(x, axis, dim):
+    ways, here, step = (lax.axis_size(axis), lax.axis_index(axis), x.shape[dim])
+    lengths = [n * ways if d == dim else n for d, n in enumerate(x.shape)]
+    full = lax.dynamic_update_slice_in_dim(jnp.zeros(lengths, x.dtype), x, here * step, axis=dim)
+    for far in range(1, ways):
+        x = lax.ppermute(x, axis, [(d, (d + 1) % ways) for d in range(ways)])
+        full = lax.dynamic_update_slice_in_dim(full, x, (here - far) % ways * step, axis=dim)
+    return full
 
 
 def body(
@@ -78,11 +88,7 @@
     gate = jnp.dot(piece, gate_weight, preferred_element_type=jnp.float32)
     up = jnp.dot(piece, up_weight, preferred_element_type=jnp.float32)
     hidden = (jax.nn.silu(gate) * up).astype(jnp.bfloat16)
-    down_part = jnp.dot(
-        lax.all_gather(hidden, "blk", axis=1, tiled=True),
-        down_weight,
-        preferred_element_type=jnp.float32,
-    )
+    down_part = jnp.dot(collect(hidden, "blk", 1), down_weight, preferred_element_type=jnp.float32)
     down_total = lax.psum(down_part.astype(jnp.bfloat16), "head").astype(jnp.float32)
     return (stream + down_total).astype(jnp.bfloat16)
 

time: 445 us -> 515 us (1.16)
  waiting for transfers between devices: 289 us -> 359 us
    ppermute x0 -> x15, waiting for transfers between devices: none -> 131 us  [collect(): x = lax.ppermute(x, axis, [(d, (d + 1) % ways) for d in range(ways)])]
    all_gather x1 -> x0, waiting for transfers between devices: 59.2 us -> none  [body(): lax.all_gather(hidden, 'blk', axis=1, tiled=True)]
    all_to_all x1, waiting for transfers between devices: 0.01 us -> 5.69 us  [body(): lax.all_to_all(row_sum[None], 'blk', split_axis=1, concat_axis=0, tiled=T...]
    all_to_all x1, waiting for transfers between devices: 5.62 us -> 0.01 us  [body(): lax.all_to_all(row_max[None], 'blk', split_axis=1, concat_axis=0, tiled=T...]
  transfers between devices with their start and end apart: 9 -> 23, of which waited for: 8 -> 22; matrix products, arithmetic and copies ran while one was open for 5% -> 4% of each run, Pallas kernels for 0% -> 0%
where the time goes in v1:
time: 515 us
  waiting for transfers between devices  359 us (70%)
  matrix products  52 us (10%)
  blocking collectives  42 us (8%)
  other arithmetic  23.8 us (5%)
  starting transfers between devices  16.5 us (3%)
  between operations  13.5 us (3%)
  local copies, waits for them, and re-layouts  8.16 us (2%)
    ppermute x15, waiting for transfers between devices, collect(): x = lax.ppermute(x, axis, [(d, (d + 1) % ways) for d in range(ways)])  131 us
    all_gather x1, waiting for transfers between devices, body(): all_queries = lax.all_gather(queries, 'blk', axis=0, tiled=True)  59.7 us
    all_gather x1, waiting for transfers between devices, body(): piece = lax.all_gather(normed, 'blk', axis=1, tiled=True)  56.9 us
    all_gather x1, waiting for transfers between devices, body(): lax.all_gather(attn, 'blk', axis=0, tiled=True)  54.4 us
    psum x1, blocking collectives, body(): squares = lax.psum(jnp.sum(stream * stream, axis=1), 'blk')  42 us
    all_to_all x1, waiting for transfers between devices, body(): lax.all_to_all(row_mean[None], 'blk', split_axis=1, concat_axis=0, tiled=...  19.9 us
    dot_general x1, matrix products, body(): jnp.einsum('bqkgd,bckd->bqkgc', shaped, key_cache, preferred_element_type...  17 us
    psum x1, waiting for transfers between devices, body(): lax.psum(proj_part.astype(jnp.bfloat16), 'head').astype(jnp.float32)  16.8 us
  transfers between devices with their start and end apart: 23, of which 22 were waited for; matrix products, arithmetic and copies ran while one was open for 4% of the time, Pallas kernels for 0%

profile of v1, /device:TPU:0, one launch (start us, length us, event | category | flops | bytes accessed | tf_op | source)
XLA Modules:
  0.0 514.5 jit_solution(9516726240578166572)
XLA Ops:
  6.5 0.7 all-gather.4.cloned.1.call-update
  7.3 0.7 iota_add_fusion.1
  8.0 0.2 broadcast_compare_fusion
  8.2 59.7 %all-gather.4.cloned.1.call-done = bf16[128,4096]{1,0:T(8,128)(2,1)} async-done(((bf16[8,4096]{1,0:T(8,128)(2,1)}), bf16[128,4096]{1,0:T(8,128)(2,1)}) %all-gather.4.cloned.1.call-update) | async-done | bytes 1048592 | tf_op jit(solution)/shard_map/all_gather | solution.py:41
  67.9 1.5 copy.45
  69.4 17.0 %fusion = (f32[2,64,4,8]{1,3,2,0:T(8,128)S(1)}, f32[2,4,2048,64,8]{2,3,4,1,0:T(8,128)}) fusion(pred[2,64,2048]{2,1,0:T(8,128)(4,1)S(1)} %broadcast_compare_fusion, bf16[2,64,4,8,128]{4,3,2,1,0:T(8,128)(2,1)S(1)} %bitcast.53, bf16[2,2048,4,128,1]{3,2,1,0,4:T(4,128)(2,1)} %bitcast.55), kind=kOutput, calls=%fused_computation.2 | convolution fusion | flops 2172645376 | bytes 39075840 | tf_op jit(solution)/shard_map/bqkgd,bckd->bqkgc/dot_general | solution.py:43
  86.4 15.1 %fusion.3 = f32[2,64,4,8]{1,3,2,0:T(8,128)S(1)} fusion(f32[2,4,2048,64,8]{2,3,4,1,0:T(8,128)} %get-tuple-element.8, f32[2,64,4,8]{1,3,2,0:T(8,128)S(1)} %get-tuple-element.7, pred[2,64,2048]{2,1,0:T(8,128)(4,1)S(1)} %broadcast_compare_fusion), kind=kLoop, calls=%fused_computation.5 | loop fusion | flops 33550336 | bytes 33849344 | tf_op jit(solution)/shard_map/reduce_sum | solution.py:51
  101.6 0.1 broadcast_in_dim_reshape.10
  101.7 0.1 copy.36
  101.8 0.5 broadcast.73
  102.2 0.7 reduce
  102.9 0.7 reshape.80
  103.6 4.5 all-to-all-start.1
  108.2 0.1 broadcast_in_dim_reshape.11
  108.3 0.1 copy.38
  108.4 0.7 reduce.2
  109.1 0.7 reshape.82
  109.8 5.7 %all-to-all-done.1 = f32[16,1,256]{2,1,0:T(1,128)S(1)} async-done(((f32[16,1,256]{2,1,0:T(1,128)}), f32[16,1,256]{2,1,0:T(1,128)S(1)}, u32[]{:S(2)}, u32[]{:S(2)}) %all-to-all-start.1) | async-done | bytes 16416 | tf_op jit(solution)/shard_map/all_to_all | solution.py:64
  115.5 3.4 all-to-all-start.2
  118.9 15.6 %fusion.12 = bf16[2,64,4,8,128]{4,1,3,2,0:T(8,128)(2,1)S(1)} fusion(bf16[2,2048,4,128,1]{3,2,1,0,4:T(4,128)(2,1)} %bitcast.63, f32[2,4,2048,64,8]{2,3,4,1,0:T(8,128)} %get-tuple-element.8, f32[2,64,4,8]{1,3,2,0:T(8,128)S(1)} %get-tuple-element.7, pred[2,64,2048]{2,1,0:T(8,128)(4,1)S(1)} %broadcast_compare_fusion, f32[2,64,4,8]{1,3,2,0:T(8,128)S(1)} %broadcast_maximum_fusion), kind=kOutput, calls=%fused_computation.15 | convolution fusion | flops 2182086656 | bytes 39092224 | tf_op jit(solution)/shard_map/bqkgc,bckd->bqkgd/dot_general | solution.py:52
  134.5 1.6 copy.33
  136.2 6.9 %all-to-all-start = ((bf16[1,128,32,128]{3,2,0,1:T(8,128)(2,1)}), bf16[1,128,32,128]{3,2,0,1:T(8,128)(2,1)S(1)}, u32[]{:S(2)}, u32[]{:S(2)}) async-start(bf16[1,128,32,128]{3,2,0,1:T(8,128)(2,1)} %bitcast.5), calls=%async_computation | async-start | bytes 2097152 | tf_op jit(solution)/shard_map/all_to_all | solution.py:66
  143.1 0.2 all-gather.6.cloned.1.call-start
  143.3 0.6 reduce.1
  143.9 0.1 reshape.81
  144.0 0.6 reduce.3
  144.6 0.1 reshape.83
  144.8 19.9 %all-to-all-done = bf16[1,128,32,128]{3,2,0,1:T(8,128)(2,1)S(1)} async-done(((bf16[1,128,32,128]{3,2,0,1:T(8,128)(2,1)}), bf16[1,128,32,128]{3,2,0,1:T(8,128)(2,1)S(1)}, u32[]{:S(2)}, u32[]{:S(2)}) %all-to-all-start) | async-done | bytes 1048608 | tf_op jit(solution)/shard_map/all_to_all | solution.py:66
  164.7 0.7 fusion.11
  165.4 0.1 fusion.19
  165.5 0.7 copy.60
  166.2 0.0 all-reduce.3.cloned.1.call-start
  166.3 54.4 %all-gather.6.cloned.1.call-done = bf16[128,4096]{1,0:T(8,128)(2,1)} async-done(((bf16[8,4096]{1,0:T(8,128)(2,1)}), bf16[128,4096]{1,0:T(8,128)(2,1)}) %all-gather.6.cloned.1.call-update) | async-done | bytes 1048592 | tf_op jit(solution)/shard_map/all_gather | solution.py:77
  220.6 3.9 convolution_convert_fusion
  224.5 0.0 all-gather.8.cloned.1.call-start
  224.6 16.8 %all-reduce.3.cloned.1.call-done = bf16[128,512]{1,0:T(8,128)(2,1)} async-done(((bf16[128,512]{1,0:T(8,128)(2,1)}), bf16[128,512]{1,0:T(8,128)(2,1)}) %all-reduce.3.cloned.1.call-update) | async-done | bytes 131088 | tf_op jit(solution)/shard_map/psum | solution.py:81
  241.4 1.0 multiply_reduce_fusion
  242.5 42.0 %psum.22 = f32[128]{0:T(128)S(1)} all-reduce(f32[128]{0:T(128)S(1)} %multiply_reduce_fusion), channel_id=1, replica_groups=mesh['groups'=1,'blk'=16,'head'=2] {'blk'}, use_global_device_ids=true, to_apply=%region_7.8 | all-reduce | flops 128 | bytes 1024 | tf_op jit(solution)/shard_map/psum | solution.py:83
  284.5 1.7 multiply_convert_fusion
  286.2 0.0 all-reduce.5.cloned.1.call-start
  286.2 56.9 %all-gather.8.cloned.1.call-done = bf16[128,8192]{1,0:T(8,128)(2,1)} async-done(((bf16[128,512]{1,0:T(8,128)(2,1)}), bf16[128,8192]{1,0:T(8,128)(2,1)}) %all-gather.8.cloned.1.call-update) | async-done | bytes 2097168 | tf_op jit(solution)/shard_map/all_gather | solution.py:87
  343.1 5.3 %fusion.23 = f32[128,512]{1,0:T(8,128)S(1)} fusion(bf16[128,8192]{1,0:T(8,128)(2,1)} %all-gather.8.cloned.1.call-done, bf16[8192,512]{1,0:T(8,128)(2,1)} %param.17), kind=kOutput, calls=%fused_computation.53 | convolution fusion | flops 1073741824 | bytes 10747904 | tf_op jit(solution)/shard_map/dot_general | solution.py:88
  348.3 0.2 broadcast_in_dim.35
  348.6 1.4 copy-done
  349.9 4.8 constant_dynamic-update-slice_fusion.15
  354.7 1.4 collective-permute-start
  356.1 7.2 %collective-permute-done = bf16[128,512]{1,0:T(8,128)(2,1)S(1)} collective-permute-done((bf16[128,512]{1,0:T(8,128)(2,1)S(1)}, bf16[128,512]{1,0:T(8,128)(2,1)S(1)}, u32[]{:S(2)}, u32[]{:S(2)}) %collective-permute-start) | collective-permute-done | bytes 131104 | tf_op jit(solution)/shard_map/ppermute | solution.py:16
  363.3 8.6 %collective-permute-done.1 = bf16[128,512]{1,0:T(8,128)(2,1)S(1)} collective-permute-done((bf16[128,512]{1,0:T(8,128)(2,1)S(1)}, bf16[128,512]{1,0:T(8,128)(2,1)S(1)}, u32[]{:S(2)}, u32[]{:S(2)}) %collective-permute-start.1) | collective-permute-done | bytes 131104 | tf_op jit(solution)/shard_map/ppermute | solution.py:16
  371.9 8.6 %collective-permute-done.2 = bf16[128,512]{1,0:T(8,128)(2,1)S(1)} collective-permute-done((bf16[128,512]{1,0:T(8,128)(2,1)S(1)}, bf16[128,512]{1,0:T(8,128)(2,1)S(1)}, u32[]{:S(2)}, u32[]{:S(2)}) %collective-permute-start.2) | collective-permute-done | bytes 131104 | tf_op jit(solution)/shard_map/ppermute | solution.py:16
  380.5 9.1 %collective-permute-done.3 = bf16[128,512]{1,0:T(8,128)(2,1)S(1)} collective-permute-done((bf16[128,512]{1,0:T(8,128)(2,1)S(1)}, bf16[128,512]{1,0:T(8,128)(2,1)S(1)}, u32[]{:S(2)}, u32[]{:S(2)}) %collective-permute-start.3) | collective-permute-done | bytes 131104 | tf_op jit(solution)/shard_map/ppermute | solution.py:16
  389.6 9.7 %collective-permute-done.4 = bf16[128,512]{1,0:T(8,128)(2,1)S(1)} collective-permute-done((bf16[128,512]{1,0:T(8,128)(2,1)S(1)}, bf16[128,512]{1,0:T(8,128)(2,1)S(1)}, u32[]{:S(2)}, u32[]{:S(2)}) %collective-permute-start.4) | collective-permute-done | bytes 131104 | tf_op jit(solution)/shard_map/ppermute | solution.py:16
  399.2 8.8 %collective-permute-done.5 = bf16[128,512]{1,0:T(8,128)(2,1)S(1)} collective-permute-done((bf16[128,512]{1,0:T(8,128)(2,1)S(1)}, bf16[128,512]{1,0:T(8,128)(2,1)S(1)}, u32[]{:S(2)}, u32[]{:S(2)}) %collective-permute-start.5) | collective-permute-done | bytes 131104 | tf_op jit(solution)/shard_map/ppermute | solution.py:16
  408.1 8.6 %collective-permute-done.6 = bf16[128,512]{1,0:T(8,128)(2,1)S(1)} collective-permute-done((bf16[128,512]{1,0:T(8,128)(2,1)S(1)}, bf16[128,512]{1,0:T(8,128)(2,1)S(1)}, u32[]{:S(2)}, u32[]{:S(2)}) %collective-permute-start.6) | collective-permute-done | bytes 131104 | tf_op jit(solution)/shard_map/ppermute | solution.py:16
  416.6 8.6 %collective-permute-done.7 = bf16[128,512]{1,0:T(8,128)(2,1)S(1)} collective-permute-done((bf16[128,512]{1,0:T(8,128)(2,1)S(1)}, bf16[128,512]{1,0:T(8,128)(2,1)S(1)}, u32[]{:S(2)}, u32[]{:S(2)}) %collective-permute-start.7) | collective-permute-done | bytes 131104 | tf_op jit(solution)/shard_map/ppermute | solution.py:16
  425.3 8.5 %collective-permute-done.8 = bf16[128,512]{1,0:T(8,128)(2,1)S(1)} collective-permute-done((bf16[128,512]{1,0:T(8,128)(2,1)S(1)}, bf16[128,512]{1,0:T(8,128)(2,1)S(1)}, u32[]{:S(2)}, u32[]{:S(2)}) %collective-permute-start.8) | collective-permute-done | bytes 131104 | tf_op jit(solution)/shard_map/ppermute | solution.py:16
  433.8 8.5 %collective-permute-done.9 = bf16[128,512]{1,0:T(8,128)(2,1)S(1)} collective-permute-done((bf16[128,512]{1,0:T(8,128)(2,1)S(1)}, bf16[128,512]{1,0:T(8,128)(2,1)S(1)}, u32[]{:S(2)}, u32[]{:S(2)}) %collective-permute-start.9) | collective-permute-done | bytes 131104 | tf_op jit(solution)/shard_map/ppermute | solution.py:16
  442.4 9.1 %collective-permute-done.10 = bf16[128,512]{1,0:T(8,128)(2,1)S(1)} collective-permute-done((bf16[128,512]{1,0:T(8,128)(2,1)S(1)}, bf16[128,512]{1,0:T(8,128)(2,1)S(1)}, u32[]{:S(2)}, u32[]{:S(2)}) %collective-permute-start.10) | collective-permute-done | bytes 131104 | tf_op jit(solution)/shard_map/ppermute | solution.py:16
  451.5 9.6 %collective-permute-done.11 = bf16[128,512]{1,0:T(8,128)(2,1)S(1)} collective-permute-done((bf16[128,512]{1,0:T(8,128)(2,1)S(1)}, bf16[128,512]{1,0:T(8,128)(2,1)S(1)}, u32[]{:S(2)}, u32[]{:S(2)}) %collective-permute-start.11) | collective-permute-done | bytes 131104 | tf_op jit(solution)/shard_map/ppermute | solution.py:16
  461.2 8.7 %collective-permute-done.12 = bf16[128,512]{1,0:T(8,128)(2,1)S(1)} collective-permute-done((bf16[128,512]{1,0:T(8,128)(2,1)S(1)}, bf16[128,512]{1,0:T(8,128)(2,1)S(1)}, u32[]{:S(2)}, u32[]{:S(2)}) %collective-permute-start.12) | collective-permute-done | bytes 131104 | tf_op jit(solution)/shard_map/ppermute | solution.py:16
  470.0 8.5 %collective-permute-done.13 = bf16[128,512]{1,0:T(8,128)(2,1)S(1)} collective-permute-done((bf16[128,512]{1,0:T(8,128)(2,1)S(1)}, bf16[128,512]{1,0:T(8,128)(2,1)S(1)}, u32[]{:S(2)}, u32[]{:S(2)}) %collective-permute-start.13) | collective-permute-done | bytes 131104 | tf_op jit(solution)/shard_map/ppermute | solution.py:16
  478.5 8.5 %collective-permute-done.14 = bf16[128,512]{1,0:T(8,128)(2,1)S(1)} collective-permute-done((bf16[128,512]{1,0:T(8,128)(2,1)S(1)}, bf16[128,512]{1,0:T(8,128)(2,1)S(1)}, u32[]{:S(2)}, u32[]{:S(2)}) %collective-permute-start.14) | collective-permute-done | bytes 131104 | tf_op jit(solution)/shard_map/ppermute | solution.py:16
  487.1 5.3 %convolution_convert_fusion.1 = bf16[128,512]{1,0:T(8,128)(2,1)} fusion(bf16[128,8192]{1,0:T(8,128)(2,1)S(1)} %constant_dynamic-update-slice_fusion, bf16[8192,512]{1,0:T(8,128)(2,1)} %param.19), kind=kOutput, calls=%fused_computation.19 | convolution fusion | flops 1073807360 | bytes 10616832 | tf_op jit(solution)/shard_map/dot_general | solution.py:91
  492.4 13.9 %all-reduce.5.cloned.1.call-done = bf16[128,512]{1,0:T(8,128)(2,1)} async-done(((bf16[128,512]{1,0:T(8,128)(2,1)}), bf16[128,512]{1,0:T(8,128)(2,1)}) %all-reduce.5.cloned.1.call-update) | async-done | bytes 131088 | tf_op jit(solution)/shard_map/psum | solution.py:92
  506.4 1.6 add_convert_fusion
  (50 shorter events, 0.5 us)
Async XLA Ops:
  6.5 61.4 %all-gather.4.cloned.1.call-start = ((), (), s32[]{:S(2)}) async-start(), calls=%async_computation.3 | async-start | bytes 1114112 | tf_op jit(solution)/shard_map/all_gather | solution.py:41
  103.6 11.8 %all-to-all-start.1 = ((f32[16,1,256]{2,1,0:T(1,128)}), f32[16,1,256]{2,1,0:T(1,128)S(1)}, u32[]{:S(2)}, u32[]{:S(2)}) async-start(f32[16,1,256]{2,1,0:T(1,128)} %reshape.80), calls=%async_computation.1 | async-start | bytes 32768 | tf_op jit(solution)/shard_map/all_to_all | solution.py:64
  115.5 20.7 %all-to-all-start.2 = ((f32[16,1,256]{2,1,0:T(1,128)}), f32[16,1,256]{2,1,0:T(1,128)S(1)}, u32[]{:S(2)}, u32[]{:S(2)}) async-start(f32[16,1,256]{2,1,0:T(1,128)} %reshape.82), calls=%async_computation.2 | async-start | bytes 32768 | tf_op jit(solution)/shard_map/all_to_all | solution.py:63
  136.2 28.5 %all-to-all-start = ((bf16[1,128,32,128]{3,2,0,1:T(8,128)(2,1)}), bf16[1,128,32,128]{3,2,0,1:T(8,128)(2,1)S(1)}, u32[]{:S(2)}, u32[]{:S(2)}) async-start(bf16[1,128,32,128]{3,2,0,1:T(8,128)(2,1)} %bitcast.5), calls=%async_computation | async-start | bytes 2097152 | tf_op jit(solution)/shard_map/all_to_all | solution.py:66
  143.1 77.6 %all-gather.6.cloned.1.call-start = ((), (), s32[]{:S(2)}) async-start(), calls=%async_computation.4 | async-start | bytes 1114112 | tf_op jit(solution)/shard_map/all_gather | solution.py:77
  166.2 58.4 %copy-start.3 = (bf16[512]{0:T(512)(128)(2,1)S(1)}, bf16[512]{0:T(512)(128)(2,1)}, u32[]{:S(2)}) copy-start(bf16[512]{0:T(512)(128)(2,1)} %param.16) | copy-start | bytes 3076
  166.2 75.2 %copy-start.1 = (bf16[128,512]{1,0:T(8,128)(2,1)S(1)}, bf16[128,512]{1,0:T(8,128)(2,1)}, u32[]{:S(2)}) copy-start(bf16[128,512]{1,0:T(8,128)(2,1)} %param.14) | copy-start | bytes 393220
  166.2 75.2 %all-reduce.3.cloned.1.call-start = ((), (), s32[]{:S(2)}) async-start(), calls=%async_computation.5 | async-start | bytes 262144 | tf_op jit(solution)/shard_map/psum | solution.py:81
  224.5 118.5 %all-gather.8.cloned.1.call-start = ((), (), s32[]{:S(2)}) async-start(), calls=%async_computation.6 | async-start | bytes 2228224 | tf_op jit(solution)/shard_map/all_gather | solution.py:87
  286.2 220.2 %all-reduce.5.cloned.1.call-start = ((), (), s32[]{:S(2)}) async-start(), calls=%async_computation.7 | async-start | bytes 262144 | tf_op jit(solution)/shard_map/psum | solution.py:92
  348.3 1.6 copy-start
  354.7 8.6 %collective-permute-start = (bf16[128,512]{1,0:T(8,128)(2,1)S(1)}, bf16[128,512]{1,0:T(8,128)(2,1)S(1)}, u32[]{:S(2)}, u32[]{:S(2)}) collective-permute-start(bf16[128,512]{1,0:T(8,128)(2,1)S(1)} %get-tuple-element.10), channel_id=1, source_target_pairs={{0,2},{2,4},{4,6},{6,8},{8,10},{10,12},{12,14},{14,16},{16,18},{18... | collective-permute-start | bytes 393224 | tf_op jit(solution)/shard_map/ppermute | solution.py:16
  363.3 8.6 %collective-permute-start.1 = (bf16[128,512]{1,0:T(8,128)(2,1)S(1)}, bf16[128,512]{1,0:T(8,128)(2,1)S(1)}, u32[]{:S(2)}, u32[]{:S(2)}) collective-permute-start(bf16[128,512]{1,0:T(8,128)(2,1)S(1)} %collective-permute-done), channel_id=1, source_target_pairs={{0,2},{2,4},{4,6},{6,8},{8,10},{10,12},{12,14},{14,16},{16,18},{18... | collective-permute-start | bytes 393224 | tf_op jit(solution)/shard_map/ppermute | solution.py:16
  371.9 8.6 %collective-permute-start.2 = (bf16[128,512]{1,0:T(8,128)(2,1)S(1)}, bf16[128,512]{1,0:T(8,128)(2,1)S(1)}, u32[]{:S(2)}, u32[]{:S(2)}) collective-permute-start(bf16[128,512]{1,0:T(8,128)(2,1)S(1)} %collective-permute-done.1), channel_id=1, source_target_pairs={{0,2},{2,4},{4,6},{6,8},{8,10},{10,12},{12,14},{14,16},{16,18},{18... | collective-permute-start | bytes 393224 | tf_op jit(solution)/shard_map/ppermute | solution.py:16
  380.5 9.1 %collective-permute-start.3 = (bf16[128,512]{1,0:T(8,128)(2,1)S(1)}, bf16[128,512]{1,0:T(8,128)(2,1)S(1)}, u32[]{:S(2)}, u32[]{:S(2)}) collective-permute-start(bf16[128,512]{1,0:T(8,128)(2,1)S(1)} %collective-permute-done.2), channel_id=1, source_target_pairs={{0,2},{2,4},{4,6},{6,8},{8,10},{10,12},{12,14},{14,16},{16,18},{18... | collective-permute-start | bytes 393224 | tf_op jit(solution)/shard_map/ppermute | solution.py:16
  389.6 9.7 %collective-permute-start.4 = (bf16[128,512]{1,0:T(8,128)(2,1)S(1)}, bf16[128,512]{1,0:T(8,128)(2,1)S(1)}, u32[]{:S(2)}, u32[]{:S(2)}) collective-permute-start(bf16[128,512]{1,0:T(8,128)(2,1)S(1)} %collective-permute-done.3), channel_id=1, source_target_pairs={{0,2},{2,4},{4,6},{6,8},{8,10},{10,12},{12,14},{14,16},{16,18},{18... | collective-permute-start | bytes 393224 | tf_op jit(solution)/shard_map/ppermute | solution.py:16
  399.2 8.8 %collective-permute-start.5 = (bf16[128,512]{1,0:T(8,128)(2,1)S(1)}, bf16[128,512]{1,0:T(8,128)(2,1)S(1)}, u32[]{:S(2)}, u32[]{:S(2)}) collective-permute-start(bf16[128,512]{1,0:T(8,128)(2,1)S(1)} %collective-permute-done.4), channel_id=1, source_target_pairs={{0,2},{2,4},{4,6},{6,8},{8,10},{10,12},{12,14},{14,16},{16,18},{18... | collective-permute-start | bytes 393224 | tf_op jit(solution)/shard_map/ppermute | solution.py:16
  408.1 8.6 %collective-permute-start.6 = (bf16[128,512]{1,0:T(8,128)(2,1)S(1)}, bf16[128,512]{1,0:T(8,128)(2,1)S(1)}, u32[]{:S(2)}, u32[]{:S(2)}) collective-permute-start(bf16[128,512]{1,0:T(8,128)(2,1)S(1)} %collective-permute-done.5), channel_id=1, source_target_pairs={{0,2},{2,4},{4,6},{6,8},{8,10},{10,12},{12,14},{14,16},{16,18},{18... | collective-permute-start | bytes 393224 | tf_op jit(solution)/shard_map/ppermute | solution.py:16
  416.6 8.6 %collective-permute-start.7 = (bf16[128,512]{1,0:T(8,128)(2,1)S(1)}, bf16[128,512]{1,0:T(8,128)(2,1)S(1)}, u32[]{:S(2)}, u32[]{:S(2)}) collective-permute-start(bf16[128,512]{1,0:T(8,128)(2,1)S(1)} %collective-permute-done.6), channel_id=1, source_target_pairs={{0,2},{2,4},{4,6},{6,8},{8,10},{10,12},{12,14},{14,16},{16,18},{18... | collective-permute-start | bytes 393224 | tf_op jit(solution)/shard_map/ppermute | solution.py:16
  425.2 8.6 %collective-permute-start.8 = (bf16[128,512]{1,0:T(8,128)(2,1)S(1)}, bf16[128,512]{1,0:T(8,128)(2,1)S(1)}, u32[]{:S(2)}, u32[]{:S(2)}) collective-permute-start(bf16[128,512]{1,0:T(8,128)(2,1)S(1)} %collective-permute-done.7), channel_id=1, source_target_pairs={{0,2},{2,4},{4,6},{6,8},{8,10},{10,12},{12,14},{14,16},{16,18},{18... | collective-permute-start | bytes 393224 | tf_op jit(solution)/shard_map/ppermute | solution.py:16
  433.8 8.6 %collective-permute-start.9 = (bf16[128,512]{1,0:T(8,128)(2,1)S(1)}, bf16[128,512]{1,0:T(8,128)(2,1)S(1)}, u32[]{:S(2)}, u32[]{:S(2)}) collective-permute-start(bf16[128,512]{1,0:T(8,128)(2,1)S(1)} %collective-permute-done.8), channel_id=1, source_target_pairs={{0,2},{2,4},{4,6},{6,8},{8,10},{10,12},{12,14},{14,16},{16,18},{18... | collective-permute-start | bytes 393224 | tf_op jit(solution)/shard_map/ppermute | solution.py:16
  442.3 9.1 %collective-permute-start.10 = (bf16[128,512]{1,0:T(8,128)(2,1)S(1)}, bf16[128,512]{1,0:T(8,128)(2,1)S(1)}, u32[]{:S(2)}, u32[]{:S(2)}) collective-permute-start(bf16[128,512]{1,0:T(8,128)(2,1)S(1)} %collective-permute-done.9), channel_id=1, source_target_pairs={{0,2},{2,4},{4,6},{6,8},{8,10},{10,12},{12,14},{14,16},{16,18},{18... | collective-permute-start | bytes 393224 | tf_op jit(solution)/shard_map/ppermute | solution.py:16
  451.5 9.6 %collective-permute-start.11 = (bf16[128,512]{1,0:T(8,128)(2,1)S(1)}, bf16[128,512]{1,0:T(8,128)(2,1)S(1)}, u32[]{:S(2)}, u32[]{:S(2)}) collective-permute-start(bf16[128,512]{1,0:T(8,128)(2,1)S(1)} %collective-permute-done.10), channel_id=1, source_target_pairs={{0,2},{2,4},{4,6},{6,8},{8,10},{10,12},{12,14},{14,16},{16,18},{18... | collective-permute-start | bytes 393224 | tf_op jit(solution)/shard_map/ppermute | solution.py:16
  461.1 8.8 %collective-permute-start.12 = (bf16[128,512]{1,0:T(8,128)(2,1)S(1)}, bf16[128,512]{1,0:T(8,128)(2,1)S(1)}, u32[]{:S(2)}, u32[]{:S(2)}) collective-permute-start(bf16[128,512]{1,0:T(8,128)(2,1)S(1)} %collective-permute-done.11), channel_id=1, source_target_pairs={{0,2},{2,4},{4,6},{6,8},{8,10},{10,12},{12,14},{14,16},{16,18},{18... | collective-permute-start | bytes 393224 | tf_op jit(solution)/shard_map/ppermute | solution.py:16
  469.9 8.6 %collective-permute-start.13 = (bf16[128,512]{1,0:T(8,128)(2,1)S(1)}, bf16[128,512]{1,0:T(8,128)(2,1)S(1)}, u32[]{:S(2)}, u32[]{:S(2)}) collective-permute-start(bf16[128,512]{1,0:T(8,128)(2,1)S(1)} %collective-permute-done.12), channel_id=1, source_target_pairs={{0,2},{2,4},{4,6},{6,8},{8,10},{10,12},{12,14},{14,16},{16,18},{18... | collective-permute-start | bytes 393224 | tf_op jit(solution)/shard_map/ppermute | solution.py:16
  478.5 8.6 %collective-permute-start.14 = (bf16[128,512]{1,0:T(8,128)(2,1)S(1)}, bf16[128,512]{1,0:T(8,128)(2,1)S(1)}, u32[]{:S(2)}, u32[]{:S(2)}) collective-permute-start(bf16[128,512]{1,0:T(8,128)(2,1)S(1)} %collective-permute-done.13), channel_id=1, source_target_pairs={{0,2},{2,4},{4,6},{6,8},{8,10},{10,12},{12,14},{14,16},{16,18},{18... | collective-permute-start | bytes 393224 | tf_op jit(solution)/shard_map/ppermute | solution.py:16
  487.1 19.3 %copy-start.2 = (bf16[128,512]{1,0:T(8,128)(2,1)S(1)}, bf16[128,512]{1,0:T(8,128)(2,1)}, u32[]{:S(2)}) copy-start(bf16[128,512]{1,0:T(8,128)(2,1)} %all-reduce.3.cloned.1.call-done) | copy-start | bytes 393220
Sparse Core Ops, SparseCore 0:
  10.1 57.7 all-gather.3
  166.3 54.2 all-gather.5
  224.7 16.7 all-reduce.2
  286.3 56.7 all-gather.7
  492.6 13.7 all-reduce.4
